TPU v7x, 32 devices: a whole 2x2x4 slice. The times are simulated.
32 devices in a mesh: parts: 2 (over y), pix: 4 (over z), par: 4 (over x, core).
Axes of the slice: x: 2, y: 2, z: 4, core: 2. Of those that a mesh axis runs over, the one named last changes fastest.
Arguments:
- green_matrix: bfloat16 [4608, 16384], P('pix', 'par'), may hold values from -0.046875 to 0.046875
- observed: bfloat16 [64, 4608], P('parts', 'pix'), parts along dimension 0, may hold values from -1000 to 1000
Outputs:
- solution: float32 [64, 16384], P('parts', 'par'), parts along dimension 0
- residual: float32 [64, 4608], P('parts', 'pix'), parts along dimension 0
There are 2 independent parts, one for each index of `parts`. A program takes and returns all parts, laid end to end along the dimension named above; an argument that names none is the same for every part. Nothing has to cross between parts.
All inputs are finite; a program needn't handle non-finite values.
Results may differ from a plain program's by a relative error of at most 0.0038.
Values may be sent and summed in bfloat16 or wider, within the bound.
No kernel may reach another device: no remote copies, remote signals or barrier semaphores. Data moves between devices by JAX's collectives and lax.ppermute only.
A program may use at most 64 MiB of HBM per device.

v0:
```python
import jax
import jax.numpy as jnp
from jax import lax
from jax.sharding import PartitionSpec as P

GRID = 128
ITERS = 5


def padded_2(block, sides, width):
    for axis, dim in sides:
        count = lax.axis_size(axis)
        forward = [(i, i + 1) for i in range(count - 1)]
        backward = [(target, source) for source, target in forward]
        low = lax.ppermute(
            lax.slice_in_dim(block, block.shape[dim] - width, None, axis=dim), axis, forward
        )
        high = lax.ppermute(lax.slice_in_dim(block, 0, width, axis=dim), axis, backward)
        block = jnp.concatenate([low, block, high], axis=dim)
    return block


def smooth(values):
    set_count = values.shape[0]
    grid_rows = values.shape[1] // GRID
    tiles = values.reshape(set_count, grid_rows, GRID)
    padded = padded_2(tiles, (("par", 1),), 1)
    padded = jnp.pad(padded, ((0, 0), (0, 0), (1, 1)))
    beside_all = (
        padded[:, 2:, 1:-1] + padded[:, :-2, 1:-1] + padded[:, 1:-1, 2:] + padded[:, 1:-1, :-2]
    )
    return (0.25 * (4.0 * tiles - beside_all)).reshape(set_count, grid_rows * GRID)


def forward(rounded, green_matrix):
    partial_value = lax.dot_general(
        rounded, green_matrix, (((1,), (1,)), ((), ())), preferred_element_type=jnp.float32
    )
    return lax.psum(partial_value, "par")


def curvatures(image, smoothed):
    local_image = jnp.sum(image * image, axis=1)
    local_smooth = jnp.sum(smoothed * smoothed, axis=1)
    image_sq = lax.psum(local_image, "pix")
    smooth_sq = lax.psum(local_smooth, "par")
    return image_sq + smooth_sq


def backward_sum(rounded, green_matrix):
    return lax.psum(jnp.dot(rounded, green_matrix, preferred_element_type=jnp.float32), "pix")


def column_squares(gradient):
    return lax.psum(jnp.sum(gradient * gradient, axis=1), "par")


def on_device(green_matrix, observed):
    set_count = observed.shape[0]
    tile_cells = green_matrix.shape[1]
    residual = observed.astype(jnp.float32)
    gradient = backward_sum(observed, green_matrix)
    grad_sq = column_squares(gradient)
    direction = gradient
    solution = jnp.zeros((set_count, tile_cells), jnp.float32)
    smooth_res = jnp.zeros((set_count, tile_cells), jnp.float32)
    for sweep in range(ITERS):
        rounded = direction.astype(jnp.bfloat16)
        image = forward(rounded, green_matrix)
        smoothed = smooth(lax.optimization_barrier(rounded).astype(jnp.float32))
        step_len = (grad_sq / curvatures(image, smoothed))[:, None]
        solution = solution + step_len * direction
        residual = residual - step_len * image
        smooth_res = smooth_res - step_len * smoothed
        if sweep + 1 < ITERS:
            gradient = backward_sum(residual.astype(jnp.bfloat16), green_matrix) + smooth(
                smooth_res
            )
            fresh_sq = column_squares(gradient)
            direction = gradient + (fresh_sq / grad_sq)[:, None] * direction
            grad_sq = fresh_sq
    return (solution, residual)


def solution(mesh):
    return jax.shard_map(
        on_device,
        mesh=mesh,
        in_specs=(P("pix", "par"), P("parts", "pix")),
        out_specs=(P("parts", "par"), P("parts", "pix")),
        check_vma=False,
    )
```

profile of v0, /device:TPU:0, one launch (start us, length us, event | category | flops | bytes accessed | tf_op | source)
XLA Modules:
  0.0 557.3 jit_solution(6629463593647099205)
XLA Ops:
  7.2 6.3 %fusion.53 = f32[32,4096]{1,0:T(8,128)} fusion(bf16[32,1152]{1,0:T(8,128)(2,1)} %param.3, bf16[1152,4096]{1,0:T(8,128)(2,1)} %param.2), kind=kOutput, calls=%fused_computation.150 | convolution fusion | flops 301989888 | bytes 10035200 | tf_op jit(solution)/shard_map/dot_general | solution.py:51
  13.5 41.3 %all-reduce.21.cloned.1.call-done = f32[32,4096]{1,0:T(8,128)} async-done(((f32[32,4096]{1,0:T(8,128)}), f32[32,4096]{1,0:T(8,128)}) %all-reduce.21.cloned.1.call-update) | async-done | bytes 524304 | tf_op jit(solution)/shard_map/psum | solution.py:51
  59.0 7.2 %fusion.54 = f32[32,1152]{1,0:T(8,128)} fusion(bf16[32,4096]{1,0:T(8,128)(2,1)S(1)} %get-tuple-element.45, bf16[1152,4096]{1,0:T(8,128)(2,1)} %param.2), kind=kOutput, calls=%fused_computation.151 | convolution fusion | flops 301989888 | bytes 9846784 | tf_op jit(solution)/shard_map/dot_general | solution.py:36
  67.5 8.5 %all-reduce.9 = (f32[32]{0:T(128)S(1)}, f32[32]{0:T(128)S(1)}) all-reduce(f32[32]{0:T(128)S(1)} %get-tuple-element.44, f32[32]{0:T(128)S(1)} %get-tuple-element.24), channel_id=1, replica_groups=mesh['parts'=2,'pix'=4,'par'=4] {'par'}, use_global_device_ids=true, to_apply=%region_2.0 | all-reduce | flops 64 | bytes 512 | tf_op jit(solution)/shard_map/psum | solution.py:55
  75.9 24.4 %all-reduce.23.cloned.1.call-done = f32[32,1152]{1,0:T(8,128)} async-done(((f32[32,1152]{1,0:T(8,128)}), f32[32,1152]{1,0:T(8,128)}) %all-reduce.23.cloned.1.call-update) | async-done | bytes 147472 | tf_op jit(solution)/shard_map/psum | solution.py:39
  101.3 11.7 %psum.178 = f32[32]{0:T(128)S(1)} all-reduce(f32[32]{0:T(128)S(1)} %multiply_reduce_fusion.13), channel_id=1, replica_groups=mesh['parts'=2,'pix'=4,'par'=4] {'pix'}, use_global_device_ids=true, to_apply=%region_5.6 | all-reduce | flops 32 | bytes 256 | tf_op jit(solution)/shard_map/psum | solution.py:45
  113.0 6.4 %fusion.28 = f32[32,4096]{1,0:T(8,128)} fusion(bf16[1152,4096]{1,0:T(8,128)(2,1)} %param.2, f32[32,1152]{1,0:T(8,128)} %all-reduce.23.cloned.1.call-done, bf16[32,1152]{1,0:T(8,128)(2,1)S(1)} %copy-done.9, f32[32]{0:T(128)S(1)} %get-tuple-element.23), kind=kOutput, calls=%fused_computation.121 | convolution fusion | flops 302137344 | bytes 10182784 | tf_op jit(solution)/shard_map/dot_general | solution.py:51
  122.2 3.3 collective-permute-done.2
  126.5 29.6 %all-reduce.25.cloned.1.call-done = f32[32,4096]{1,0:T(8,128)} async-done(((f32[32,4096]{1,0:T(8,128)}), f32[32,4096]{1,0:T(8,128)}) %all-reduce.25.cloned.1.call-update) | async-done | bytes 524304 | tf_op jit(solution)/shard_map/psum | solution.py:51
  156.1 1.5 multiply_reduce_fusion.6
  157.6 5.7 %psum.181 = f32[32]{0:T(128)S(1)} all-reduce(f32[32]{0:T(128)S(1)} %multiply_reduce_fusion.6), channel_id=1, replica_groups=mesh['parts'=2,'pix'=4,'par'=4] {'par'}, use_global_device_ids=true, to_apply=%region_10.11 | all-reduce | flops 32 | bytes 256 | tf_op jit(solution)/shard_map/psum | solution.py:55
  163.8 1.8 collective-permute-start.5
  166.9 7.2 %fusion.55 = f32[32,1152]{1,0:T(8,128)} fusion(bf16[32,4096]{1,0:T(8,128)(2,1)S(1)} %get-tuple-element.20, bf16[1152,4096]{1,0:T(8,128)(2,1)} %param.2), kind=kOutput, calls=%fused_computation.152 | convolution fusion | flops 301989888 | bytes 9846784 | tf_op jit(solution)/shard_map/dot_general | solution.py:36
  175.4 8.4 %psum.184 = f32[32]{0:T(128)S(1)} all-reduce(f32[32]{0:T(128)S(1)} %get-tuple-element.18), channel_id=1, replica_groups=mesh['parts'=2,'pix'=4,'par'=4] {'par'}, use_global_device_ids=true, to_apply=%region_15.16 | all-reduce | flops 32 | bytes 256 | tf_op jit(solution)/shard_map/psum | solution.py:46
  183.8 24.2 %all-reduce.27.cloned.1.call-done = f32[32,1152]{1,0:T(8,128)} async-done(((f32[32,1152]{1,0:T(8,128)}), f32[32,1152]{1,0:T(8,128)}) %all-reduce.27.cloned.1.call-update) | async-done | bytes 147472 | tf_op jit(solution)/shard_map/psum | solution.py:39
  209.0 11.7 %psum.183 = f32[32]{0:T(128)S(1)} all-reduce(f32[32]{0:T(128)S(1)} %multiply_reduce_fusion.12), channel_id=1, replica_groups=mesh['parts'=2,'pix'=4,'par'=4] {'pix'}, use_global_device_ids=true, to_apply=%region_13.14 | all-reduce | flops 32 | bytes 256 | tf_op jit(solution)/shard_map/psum | solution.py:45
  221.7 6.2 %fusion.34 = f32[32,4096]{1,0:T(8,128)} fusion(bf16[1152,4096]{1,0:T(8,128)(2,1)} %param.2, f32[32,1152]{1,0:T(8,128)S(1)} %multiply_subtract_fusion.7), kind=kOutput, calls=%fused_computation.126 | convolution fusion | flops 302026752 | bytes 10108928 | tf_op jit(solution)/shard_map/dot_general | solution.py:51
  230.8 3.3 collective-permute-done.6
  235.0 29.6 %all-reduce.29.cloned.1.call-done = f32[32,4096]{1,0:T(8,128)} async-done(((f32[32,4096]{1,0:T(8,128)}), f32[32,4096]{1,0:T(8,128)}) %all-reduce.29.cloned.1.call-update) | async-done | bytes 524304 | tf_op jit(solution)/shard_map/psum | solution.py:51
  264.6 1.5 multiply_reduce_fusion.4
  266.1 5.7 %psum.186 = f32[32]{0:T(128)S(1)} all-reduce(f32[32]{0:T(128)S(1)} %multiply_reduce_fusion.4), channel_id=1, replica_groups=mesh['parts'=2,'pix'=4,'par'=4] {'par'}, use_global_device_ids=true, to_apply=%region_18.19 | all-reduce | flops 32 | bytes 256 | tf_op jit(solution)/shard_map/psum | solution.py:55
  272.4 1.8 collective-permute-start.9
  275.4 7.2 %fusion.56 = f32[32,1152]{1,0:T(8,128)} fusion(bf16[32,4096]{1,0:T(8,128)(2,1)S(1)} %get-tuple-element.14, bf16[1152,4096]{1,0:T(8,128)(2,1)} %param.2), kind=kOutput, calls=%fused_computation.153 | convolution fusion | flops 301989888 | bytes 9846784 | tf_op jit(solution)/shard_map/dot_general | solution.py:36
  283.9 8.3 %psum.189 = f32[32]{0:T(128)S(1)} all-reduce(f32[32]{0:T(128)S(1)} %get-tuple-element.12), channel_id=1, replica_groups=mesh['parts'=2,'pix'=4,'par'=4] {'par'}, use_global_device_ids=true, to_apply=%region_23.24 | all-reduce | flops 32 | bytes 256 | tf_op jit(solution)/shard_map/psum | solution.py:46
  292.1 24.4 %all-reduce.31.cloned.1.call-done = f32[32,1152]{1,0:T(8,128)} async-done(((f32[32,1152]{1,0:T(8,128)}), f32[32,1152]{1,0:T(8,128)}) %all-reduce.31.cloned.1.call-update) | async-done | bytes 147472 | tf_op jit(solution)/shard_map/psum | solution.py:39
  317.5 11.7 %psum.188 = f32[32]{0:T(128)S(1)} all-reduce(f32[32]{0:T(128)S(1)} %multiply_reduce_fusion.11), channel_id=1, replica_groups=mesh['parts'=2,'pix'=4,'par'=4] {'pix'}, use_global_device_ids=true, to_apply=%region_21.22 | all-reduce | flops 32 | bytes 256 | tf_op jit(solution)/shard_map/psum | solution.py:45
  329.2 6.4 %fusion.32 = f32[32,4096]{1,0:T(8,128)} fusion(bf16[1152,4096]{1,0:T(8,128)(2,1)} %param.2, f32[32,1152]{1,0:T(8,128)S(1)} %multiply_subtract_fusion.7, f32[32,1152]{1,0:T(8,128)} %all-reduce.31.cloned.1.call-done, f32[32]{0:T(128)S(1)} %get-tuple-element.11), kind=kOutput, calls=%fused_computation.124 | convolution fusion | flops 302100480 | bytes 10256512 | tf_op jit(solution)/shard_map/dot_general | solution.py:51
  338.5 3.3 collective-permute-done.10
  342.7 29.6 %all-reduce.33.cloned.1.call-done = f32[32,4096]{1,0:T(8,128)} async-done(((f32[32,4096]{1,0:T(8,128)}), f32[32,4096]{1,0:T(8,128)}) %all-reduce.33.cloned.1.call-update) | async-done | bytes 524304 | tf_op jit(solution)/shard_map/psum | solution.py:51
  372.3 1.5 multiply_reduce_fusion.2
  373.7 5.7 %psum.191 = f32[32]{0:T(128)S(1)} all-reduce(f32[32]{0:T(128)S(1)} %multiply_reduce_fusion.2), channel_id=1, replica_groups=mesh['parts'=2,'pix'=4,'par'=4] {'par'}, use_global_device_ids=true, to_apply=%region_26.27 | all-reduce | flops 32 | bytes 256 | tf_op jit(solution)/shard_map/psum | solution.py:55
  381.0 1.8 collective-permute-start.13
  382.8 1.5 collective-permute-start.12
  384.3 7.2 %fusion.57 = f32[32,1152]{1,0:T(8,128)} fusion(bf16[32,4096]{1,0:T(8,128)(2,1)S(1)} %get-tuple-element.8, bf16[1152,4096]{1,0:T(8,128)(2,1)} %param.2), kind=kOutput, calls=%fused_computation.154 | convolution fusion | flops 301989888 | bytes 9846784 | tf_op jit(solution)/shard_map/dot_general | solution.py:36
  393.4 8.3 %psum.194 = f32[32]{0:T(128)S(1)} all-reduce(f32[32]{0:T(128)S(1)} %get-tuple-element.6), channel_id=1, replica_groups=mesh['parts'=2,'pix'=4,'par'=4] {'par'}, use_global_device_ids=true, to_apply=%region_31.32 | all-reduce | flops 32 | bytes 256 | tf_op jit(solution)/shard_map/psum | solution.py:46
  401.7 23.6 %all-reduce.35.cloned.1.call-done = f32[32,1152]{1,0:T(8,128)} async-done(((f32[32,1152]{1,0:T(8,128)}), f32[32,1152]{1,0:T(8,128)}) %all-reduce.35.cloned.1.call-update) | async-done | bytes 147472 | tf_op jit(solution)/shard_map/psum | solution.py:39
  426.4 11.7 %psum.193 = f32[32]{0:T(128)S(1)} all-reduce(f32[32]{0:T(128)S(1)} %multiply_reduce_fusion.10), channel_id=1, replica_groups=mesh['parts'=2,'pix'=4,'par'=4] {'pix'}, use_global_device_ids=true, to_apply=%region_29.30 | all-reduce | flops 32 | bytes 256 | tf_op jit(solution)/shard_map/psum | solution.py:45
  439.8 6.3 %fusion.30 = f32[32,4096]{1,0:T(8,128)} fusion(bf16[1152,4096]{1,0:T(8,128)(2,1)} %param.2, f32[32,1152]{1,0:T(8,128)S(1)} %multiply_subtract_fusion.5), kind=kOutput, calls=%fused_computation.122 | convolution fusion | flops 302026752 | bytes 10108928 | tf_op jit(solution)/shard_map/dot_general | solution.py:51
  448.9 3.3 collective-permute-done.14
  453.1 29.6 %all-reduce.37.cloned.1.call-done = f32[32,4096]{1,0:T(8,128)} async-done(((f32[32,4096]{1,0:T(8,128)}), f32[32,4096]{1,0:T(8,128)}) %all-reduce.37.cloned.1.call-update) | async-done | bytes 524304 | tf_op jit(solution)/shard_map/psum | solution.py:51
  482.7 1.5 multiply_reduce_fusion
  484.2 5.7 %psum.196 = f32[32]{0:T(128)S(1)} all-reduce(f32[32]{0:T(128)S(1)} %multiply_reduce_fusion), channel_id=1, replica_groups=mesh['parts'=2,'pix'=4,'par'=4] {'par'}, use_global_device_ids=true, to_apply=%region_34.35 | all-reduce | flops 32 | bytes 256 | tf_op jit(solution)/shard_map/psum | solution.py:55
  490.5 1.8 collective-permute-start.17
  493.5 7.2 %fusion.58 = f32[32,1152]{1,0:T(8,128)} fusion(bf16[32,4096]{1,0:T(8,128)(2,1)S(1)} %fusion.26, bf16[1152,4096]{1,0:T(8,128)(2,1)} %param.2), kind=kOutput, calls=%fused_computation.155 | convolution fusion | flops 301989888 | bytes 9846784 | tf_op jit(solution)/shard_map/dot_general | solution.py:36
  501.9 8.3 %psum.199 = f32[32]{0:T(128)S(1)} all-reduce(f32[32]{0:T(128)S(1)} %fusion.4), channel_id=1, replica_groups=mesh['parts'=2,'pix'=4,'par'=4] {'par'}, use_global_device_ids=true, to_apply=%region_39.40 | all-reduce | flops 32 | bytes 256 | tf_op jit(solution)/shard_map/psum | solution.py:46
  510.2 24.4 %all-reduce.39.cloned.1.call-done = f32[32,1152]{1,0:T(8,128)} async-done(((f32[32,1152]{1,0:T(8,128)}), f32[32,1152]{1,0:T(8,128)}) %all-reduce.39.cloned.1.call-update) | async-done | bytes 147472 | tf_op jit(solution)/shard_map/psum | solution.py:39
  535.6 11.7 %psum.198 = f32[32]{0:T(128)S(1)} all-reduce(f32[32]{0:T(128)S(1)} %multiply_reduce_fusion.9), channel_id=1, replica_groups=mesh['parts'=2,'pix'=4,'par'=4] {'pix'}, use_global_device_ids=true, to_apply=%region_37.38 | all-reduce | flops 32 | bytes 256 | tf_op jit(solution)/shard_map/psum | solution.py:45
  547.4 2.4 multiply_add_fusion
  (132 shorter events, 41.2 us)
Async XLA Ops:
  7.2 47.7 %all-reduce.21.cloned.1.call-start = ((), (), s32[]{:S(2)}) async-start(), calls=%async_computation | async-start | bytes 1048576 | tf_op jit(solution)/shard_map/psum | solution.py:51
  13.5 86.8 %all-reduce.23.cloned.1.call-start = ((), (), s32[]{:S(2)}) async-start(), calls=%async_computation.1 | async-start | bytes 294912 | tf_op jit(solution)/shard_map/psum | solution.py:39
  56.4 9.9 %collective-permute-start.1 = (f32[32,1,128]{2,1,0:T(1,128)S(1)}, f32[32,1,128]{2,1,0:T(1,128)S(1)}, u32[]{:S(2)}, u32[]{:S(2)}) collective-permute-start(f32[32,1,128]{2,1,0:T(1,128)S(1)} %get-tuple-element.42), channel_id=1, source_target_pairs={{0,1},{1,2},{2,3},{4,5},{5,6},{6,7},{8,9},{9,10},{10,11},{12,13},{... | collective-permute-start | bytes 49160 | tf_op jit(solution)/shard_map/ppermute | solution.py:15
  57.7 8.6 %collective-permute-start = (f32[32,1,128]{2,1,0:T(1,128)S(1)}, f32[32,1,128]{2,1,0:T(1,128)S(1)}, u32[]{:S(2)}, u32[]{:S(2)}) collective-permute-start(f32[32,1,128]{2,1,0:T(1,128)S(1)} %get-tuple-element.43), channel_id=1, source_target_pairs={{1,0},{2,1},{3,2},{5,4},{6,5},{7,6},{9,8},{10,9},{11,10},{13,12},{... | collective-permute-start | bytes 49160 | tf_op jit(solution)/shard_map/ppermute | solution.py:18
  66.3 89.8 %all-reduce.25.cloned.1.call-start = ((), (), s32[]{:S(2)}) async-start(), calls=%async_computation.2 | async-start | bytes 1048576 | tf_op jit(solution)/shard_map/psum | solution.py:51
  66.9 46.2 %copy-start.9 = (bf16[32,1152]{1,0:T(8,128)(2,1)S(1)}, bf16[32,1152]{1,0:T(8,128)(2,1)}, u32[]{:S(2)}) copy-start(bf16[32,1152]{1,0:T(8,128)(2,1)} %param.3) | copy-start | bytes 221188
  119.4 88.6 %all-reduce.27.cloned.1.call-start = ((), (), s32[]{:S(2)}) async-start(), calls=%async_computation.3 | async-start | bytes 294912 | tf_op jit(solution)/shard_map/psum | solution.py:39
  119.6 2.6 collective-permute-start.3
  120.9 4.6 collective-permute-start.2
  126.1 37.2 %copy-start = (f32[32,4096]{1,0:T(8,128)S(1)}, f32[32,4096]{1,0:T(8,128)}, u32[]{:S(2)}) copy-start(f32[32,4096]{1,0:T(8,128)} %all-reduce.21.cloned.1.call-done) | copy-start | bytes 1572868
  156.1 7.2 %copy-start.5 = (f32[32,4096]{1,0:T(8,128)S(1)}, f32[32,4096]{1,0:T(8,128)}, u32[]{:S(2)}) copy-start(f32[32,4096]{1,0:T(8,128)} %all-reduce.25.cloned.1.call-done) | copy-start | bytes 1572868
  163.8 10.4 %collective-permute-start.5 = (f32[32,1,128]{2,1,0:T(1,128)S(1)}, f32[32,1,128]{2,1,0:T(1,128)S(1)}, u32[]{:S(2)}, u32[]{:S(2)}) collective-permute-start(f32[32,1,128]{2,1,0:T(1,128)S(1)} %get-tuple-element.38), channel_id=1, source_target_pairs={{0,1},{1,2},{2,3},{4,5},{5,6},{6,7},{8,9},{9,10},{10,11},{12,13},{... | collective-permute-start | bytes 49160 | tf_op jit(solution)/shard_map/ppermute | solution.py:15
  165.6 8.6 %collective-permute-start.4 = (f32[32,1,128]{2,1,0:T(1,128)S(1)}, f32[32,1,128]{2,1,0:T(1,128)S(1)}, u32[]{:S(2)}, u32[]{:S(2)}) collective-permute-start(f32[32,1,128]{2,1,0:T(1,128)S(1)} %get-tuple-element.39), channel_id=1, source_target_pairs={{1,0},{2,1},{3,2},{5,4},{6,5},{7,6},{9,8},{10,9},{11,10},{13,12},{... | collective-permute-start | bytes 49160 | tf_op jit(solution)/shard_map/ppermute | solution.py:18
  174.2 90.4 %all-reduce.29.cloned.1.call-start = ((), (), s32[]{:S(2)}) async-start(), calls=%async_computation.4 | async-start | bytes 1048576 | tf_op jit(solution)/shard_map/psum | solution.py:51
  174.8 45.9 %copy-start.6 = (f32[32,1152]{1,0:T(8,128)S(1)}, f32[32,1152]{1,0:T(8,128)}, u32[]{:S(2)}) copy-start(f32[32,1152]{1,0:T(8,128)} %all-reduce.23.cloned.1.call-done) | copy-start | bytes 442372
  228.0 88.5 %all-reduce.31.cloned.1.call-start = ((), (), s32[]{:S(2)}) async-start(), calls=%async_computation.5 | async-start | bytes 294912 | tf_op jit(solution)/shard_map/psum | solution.py:39
  228.2 2.6 collective-permute-start.7
  229.5 4.6 collective-permute-start.6
  264.6 7.2 %copy-start.4 = (f32[32,4096]{1,0:T(8,128)S(1)}, f32[32,4096]{1,0:T(8,128)}, u32[]{:S(2)}) copy-start(f32[32,4096]{1,0:T(8,128)} %all-reduce.29.cloned.1.call-done) | copy-start | bytes 1572868
  272.4 10.4 %collective-permute-start.9 = (f32[32,1,128]{2,1,0:T(1,128)S(1)}, f32[32,1,128]{2,1,0:T(1,128)S(1)}, u32[]{:S(2)}, u32[]{:S(2)}) collective-permute-start(f32[32,1,128]{2,1,0:T(1,128)S(1)} %get-tuple-element.34), channel_id=1, source_target_pairs={{0,1},{1,2},{2,3},{4,5},{5,6},{6,7},{8,9},{9,10},{10,11},{12,13},{... | collective-permute-start | bytes 49160 | tf_op jit(solution)/shard_map/ppermute | solution.py:15
  274.1 8.6 %collective-permute-start.8 = (f32[32,1,128]{2,1,0:T(1,128)S(1)}, f32[32,1,128]{2,1,0:T(1,128)S(1)}, u32[]{:S(2)}, u32[]{:S(2)}) collective-permute-start(f32[32,1,128]{2,1,0:T(1,128)S(1)} %get-tuple-element.35), channel_id=1, source_target_pairs={{1,0},{2,1},{3,2},{5,4},{6,5},{7,6},{9,8},{10,9},{11,10},{13,12},{... | collective-permute-start | bytes 49160 | tf_op jit(solution)/shard_map/ppermute | solution.py:18
  282.7 89.6 %all-reduce.33.cloned.1.call-start = ((), (), s32[]{:S(2)}) async-start(), calls=%async_computation.6 | async-start | bytes 1048576 | tf_op jit(solution)/shard_map/psum | solution.py:51
  335.6 89.7 %all-reduce.35.cloned.1.call-start = ((), (), s32[]{:S(2)}) async-start(), calls=%async_computation.7 | async-start | bytes 294912 | tf_op jit(solution)/shard_map/psum | solution.py:39
  335.8 2.6 collective-permute-start.11
  337.1 4.6 collective-permute-start.10
  381.0 10.6 %collective-permute-start.13 = (f32[32,1,128]{2,1,0:T(1,128)S(1)}, f32[32,1,128]{2,1,0:T(1,128)S(1)}, u32[]{:S(2)}, u32[]{:S(2)}) collective-permute-start(f32[32,1,128]{2,1,0:T(1,128)S(1)} %get-tuple-element.30), channel_id=1, source_target_pairs={{0,1},{1,2},{2,3},{4,5},{5,6},{6,7},{8,9},{9,10},{10,11},{12,13},{... | collective-permute-start | bytes 49160 | tf_op jit(solution)/shard_map/ppermute | solution.py:15
  382.8 8.8 %collective-permute-start.12 = (f32[32,1,128]{2,1,0:T(1,128)S(1)}, f32[32,1,128]{2,1,0:T(1,128)S(1)}, u32[]{:S(2)}, u32[]{:S(2)}) collective-permute-start(f32[32,1,128]{2,1,0:T(1,128)S(1)} %get-tuple-element.31), channel_id=1, source_target_pairs={{1,0},{2,1},{3,2},{5,4},{6,5},{7,6},{9,8},{10,9},{11,10},{13,12},{... | collective-permute-start | bytes 49160 | tf_op jit(solution)/shard_map/ppermute | solution.py:18
  391.5 91.2 %all-reduce.37.cloned.1.call-start = ((), (), s32[]{:S(2)}) async-start(), calls=%async_computation.8 | async-start | bytes 1048576 | tf_op jit(solution)/shard_map/psum | solution.py:51
  392.2 45.9 %copy-start.2 = (f32[32,1152]{1,0:T(8,128)S(1)}, f32[32,1152]{1,0:T(8,128)}, u32[]{:S(2)}) copy-start(f32[32,1152]{1,0:T(8,128)} %all-reduce.31.cloned.1.call-done) | copy-start | bytes 442372
  439.1 0.7 copy-start.7
  439.8 6.4 %copy-start.3 = (f32[32,32,128]{2,1,0:T(8,128)S(1)}, f32[32,32,128]{2,1,0:T(8,128)}, u32[]{:S(2)}) copy-start(f32[32,32,128]{2,1,0:T(8,128)} %get-tuple-element.7) | copy-start | bytes 1572868
  446.1 88.5 %all-reduce.39.cloned.1.call-start = ((), (), s32[]{:S(2)}) async-start(), calls=%async_computation.9 | async-start | bytes 294912 | tf_op jit(solution)/shard_map/psum | solution.py:39
  446.3 2.6 collective-permute-start.15
  447.6 4.6 collective-permute-start.14
  482.7 7.2 %copy-start.1 = (f32[32,4096]{1,0:T(8,128)S(1)}, f32[32,4096]{1,0:T(8,128)}, u32[]{:S(2)}) copy-start(f32[32,4096]{1,0:T(8,128)} %all-reduce.37.cloned.1.call-done) | copy-start | bytes 1572868
  490.5 10.3 %collective-permute-start.17 = (f32[32,1,128]{2,1,0:T(1,128)S(1)}, f32[32,1,128]{2,1,0:T(1,128)S(1)}, u32[]{:S(2)}, u32[]{:S(2)}) collective-permute-start(f32[32,1,128]{2,1,0:T(1,128)S(1)} %get-tuple-element.26), channel_id=1, source_target_pairs={{0,1},{1,2},{2,3},{4,5},{5,6},{6,7},{8,9},{9,10},{10,11},{12,13},{... | collective-permute-start | bytes 49160 | tf_op jit(solution)/shard_map/ppermute | solution.py:15
  492.2 8.6 %collective-permute-start.16 = (f32[32,1,128]{2,1,0:T(1,128)S(1)}, f32[32,1,128]{2,1,0:T(1,128)S(1)}, u32[]{:S(2)}, u32[]{:S(2)}) collective-permute-start(f32[32,1,128]{2,1,0:T(1,128)S(1)} %get-tuple-element.27), channel_id=1, source_target_pairs={{1,0},{2,1},{3,2},{5,4},{6,5},{7,6},{9,8},{10,9},{11,10},{13,12},{... | collective-permute-start | bytes 49160 | tf_op jit(solution)/shard_map/ppermute | solution.py:18
  547.3 2.4 copy-start.8
  547.3 2.4 copy-start.10
Sparse Core Ops, SparseCore 0:
  13.6 41.2 all-reduce.20
  66.4 33.8 all-reduce.22
  119.6 36.4 all-reduce.24
  174.3 33.6 all-reduce.26
  228.1 36.4 all-reduce.28
  282.8 33.6 all-reduce.30
  335.8 36.4 all-reduce.32
  391.7 33.6 all-reduce.34
  446.2 36.4 all-reduce.36
  500.9 33.6 all-reduce.38
where the time goes:
time: 559 us; the launch traced here: 557 us
  waiting for transfers between devices  294 us (53%)
  blocking collectives  123 us (22%)
  matrix products  67.6 us (12%)
  other arithmetic  30.8 us (6%)
  starting transfers between devices  25.8 us (5%)
  between operations  14.8 us (3%)
    psum x5, waiting for transfers between devices, backward_sum(): lax.psum(jnp.dot(rounded, green_matrix, preferred_element_type=jnp.float3...  160 us
    psum x5, waiting for transfers between devices, forward(): return lax.psum(partial_value, 'par')  121 us
    psum x5, blocking collectives, curvatures(): image_sq = lax.psum(local_image, 'pix')  58.5 us
    dot_general x5, matrix products, forward(): lax.dot_general(rounded, green_matrix, (((1,), (1,)), ((), ())), preferre...  36.2 us
    psum x4, blocking collectives, curvatures(): smooth_sq = lax.psum(local_smooth, 'par')  33.2 us
    dot_general x5, matrix products, backward_sum(): jnp.dot(rounded, green_matrix, preferred_element_type=jnp.float32)  31.5 us
    psum x5, blocking collectives, column_squares(): return lax.psum(jnp.sum(gradient * gradient, axis=1), 'par')  31.1 us
    ppermute x9, starting transfers between devices, padded_2(): lax.ppermute(lax.slice_in_dim(block, block.shape[dim] - width, None, axis...  13.5 us
  transfers between devices with their start and end apart: 28, of which 14 were waited for; matrix products, arithmetic and copies ran while one was open for 8% of the time, Pallas kernels for 0%

commit v1 on v0

--- a/solution.py
+++ b/solution.py
@@ -36,7 +36,7 @@
     partial_value = lax.dot_general(
         rounded, green_matrix, (((1,), (1,)), ((), ())), preferred_element_type=jnp.float32
     )
-    return lax.psum(partial_value, "par")
+    return jnp.sum(lax.all_gather(partial_value, "par"), axis=0)
 
 
 def curvatures(image, smoothed):

time: 559 us -> 465 us (0.83)
  waiting for transfers between devices: 294 us -> 173 us
  blocking collectives: 123 us -> 147 us
  starting transfers between devices: 25.8 us -> 32.1 us
    psum x5 -> x0, waiting for transfers between devices: 121 us -> none  [forward(): return lax.psum(partial_value, 'par')]
    all_gather x0 -> x5, blocking collectives: none -> 39.5 us  [forward(): return jnp.sum(lax.all_gather(partial_value, 'par'), axis=0)]
    psum x4, blocking collectives: 33.2 us -> 25.7 us  [curvatures(): smooth_sq = lax.psum(local_smooth, 'par')]
    ppermute x9, starting transfers between devices: 13.5 us -> 20.3 us  [padded_2(): lax.ppermute(lax.slice_in_dim(block, block.shape[dim] - width, None, axis...]
  transfers between devices with their start and end apart: 28 -> 23, of which waited for: 14 -> 9; matrix products, arithmetic and copies ran while one was open for 8% -> 1% of each run, Pallas kernels for 0% -> 0%
where the time goes in v1:
time: 465 us; the launch traced here: 464 us
  waiting for transfers between devices  173 us (37%)
  blocking collectives  147 us (32%)
  matrix products  64.1 us (14%)
  starting transfers between devices  32.1 us (7%)
  other arithmetic  29.3 us (6%)
  between operations  14.5 us (3%)
    psum x5, waiting for transfers between devices, backward_sum(): lax.psum(jnp.dot(rounded, green_matrix, preferred_element_type=jnp.float3...  160 us
    psum x5, blocking collectives, curvatures(): image_sq = lax.psum(local_image, 'pix')  53.2 us
    all_gather x5, blocking collectives, forward(): return jnp.sum(lax.all_gather(partial_value, 'par'), axis=0)  39.5 us
    dot_general x5, matrix products, forward(): lax.dot_general(rounded, green_matrix, (((1,), (1,)), ((), ())), preferre...  32.9 us
    dot_general x5, matrix products, backward_sum(): jnp.dot(rounded, green_matrix, preferred_element_type=jnp.float32)  31.3 us
    psum x5, blocking collectives, column_squares(): return lax.psum(jnp.sum(gradient * gradient, axis=1), 'par')  29.1 us
    psum x4, blocking collectives, curvatures(): smooth_sq = lax.psum(local_smooth, 'par')  25.7 us
    ppermute x9, starting transfers between devices, padded_2(): lax.ppermute(lax.slice_in_dim(block, block.shape[dim] - width, None, axis...  20.3 us
  transfers between devices with their start and end apart: 23, of which 9 were waited for; matrix products, arithmetic and copies ran while one was open for 1% of the time, Pallas kernels for 0%

profile of v1, /device:TPU:0, one launch (start us, length us, event | category | flops | bytes accessed | tf_op | source)
XLA Modules:
  0.0 463.9 jit_solution(11283802326458597638)
XLA Ops:
  7.2 6.3 %fusion.53 = f32[32,4096]{1,0:T(8,128)} fusion(bf16[32,1152]{1,0:T(8,128)(2,1)} %param.3, bf16[1152,4096]{1,0:T(8,128)(2,1)} %param.2), kind=kOutput, calls=%fused_computation.150 | convolution fusion | flops 301989888 | bytes 10035200 | tf_op jit(solution)/shard_map/dot_general | solution.py:51
  13.5 41.3 %all-reduce.16.cloned.1.call-done = f32[32,4096]{1,0:T(8,128)} async-done(((f32[32,4096]{1,0:T(8,128)}), f32[32,4096]{1,0:T(8,128)}) %all-reduce.16.cloned.1.call-update) | async-done | bytes 524304 | tf_op jit(solution)/shard_map/psum | solution.py:51
  56.2 6.6 %fusion.54 = f32[32,1152]{1,0:T(8,128)S(1)} fusion(bf16[32,4096]{1,0:T(8,128)(2,1)S(1)} %get-tuple-element.45, bf16[1152,4096]{1,0:T(8,128)(2,1)} %param.2), kind=kOutput, calls=%fused_computation.151 | convolution fusion | flops 301989888 | bytes 9846784 | tf_op jit(solution)/shard_map/dot_general | solution.py:36
  62.8 7.5 %all-gather = f32[128,1152]{1,0:T(8,128)S(1)} all-gather(f32[32,1152]{1,0:T(8,128)S(1)} %fusion.54), channel_id=2, replica_groups=mesh['parts'=2,'pix'=4,'par'=4] {'par'}, dimensions={0}, use_global_device_ids=true | all-gather | bytes 737280 | tf_op jit(solution)/shard_map/all_gather | solution.py:39
  70.5 2.3 collective-permute-start.1
  74.2 10.6 %psum.142 = f32[32]{0:T(128)S(1)} all-reduce(f32[32]{0:T(128)S(1)} %multiply_reduce_fusion.13), channel_id=1, replica_groups=mesh['parts'=2,'pix'=4,'par'=4] {'pix'}, use_global_device_ids=true, to_apply=%region_5.6 | all-reduce | flops 32 | bytes 256 | tf_op jit(solution)/shard_map/psum | solution.py:45
  85.9 6.2 %all-reduce.9 = (f32[32]{0:T(128)S(1)}, f32[32]{0:T(128)S(1)}) all-reduce(f32[32]{0:T(128)S(1)} %get-tuple-element.44, f32[32]{0:T(128)S(1)} %get-tuple-element.24), channel_id=1, replica_groups=mesh['parts'=2,'pix'=4,'par'=4] {'par'}, use_global_device_ids=true, to_apply=%region_2.0 | all-reduce | flops 64 | bytes 512 | tf_op jit(solution)/shard_map/psum | solution.py:55
  92.1 6.3 %fusion.28 = f32[32,4096]{1,0:T(8,128)} fusion(bf16[1152,4096]{1,0:T(8,128)(2,1)} %param.2, f32[32,1152]{1,0:T(8,128)S(1)} %reduce_sum.181, bf16[32,1152]{1,0:T(8,128)(2,1)S(1)} %copy-done.11, f32[32]{0:T(128)S(1)} %get-tuple-element.23), kind=kOutput, calls=%fused_computation.121 | convolution fusion | flops 302137344 | bytes 10182784 | tf_op jit(solution)/shard_map/dot_general | solution.py:51
  98.6 2.2 collective-permute-start.3
  102.2 3.3 collective-permute-done.2
  106.4 29.7 %all-reduce.18.cloned.1.call-done = f32[32,4096]{1,0:T(8,128)} async-done(((f32[32,4096]{1,0:T(8,128)}), f32[32,4096]{1,0:T(8,128)}) %all-reduce.18.cloned.1.call-update) | async-done | bytes 524304 | tf_op jit(solution)/shard_map/psum | solution.py:51
  137.7 5.7 %psum.145 = f32[32]{0:T(128)S(1)} all-reduce(f32[32]{0:T(128)S(1)} %multiply_reduce_fusion.6), channel_id=1, replica_groups=mesh['parts'=2,'pix'=4,'par'=4] {'par'}, use_global_device_ids=true, to_apply=%region_10.11 | all-reduce | flops 32 | bytes 256 | tf_op jit(solution)/shard_map/psum | solution.py:55
  143.7 6.6 %fusion.55 = f32[32,1152]{1,0:T(8,128)S(1)} fusion(bf16[32,4096]{1,0:T(8,128)(2,1)S(1)} %get-tuple-element.20, bf16[1152,4096]{1,0:T(8,128)(2,1)} %param.2), kind=kOutput, calls=%fused_computation.152 | convolution fusion | flops 301989888 | bytes 9846784 | tf_op jit(solution)/shard_map/dot_general | solution.py:36
  150.3 7.8 %all-gather.1 = f32[128,1152]{1,0:T(8,128)S(1)} all-gather(f32[32,1152]{1,0:T(8,128)S(1)} %fusion.55), channel_id=3, replica_groups=mesh['parts'=2,'pix'=4,'par'=4] {'par'}, dimensions={0}, use_global_device_ids=true | all-gather | bytes 737280 | tf_op jit(solution)/shard_map/all_gather | solution.py:39
  158.3 2.3 collective-permute-start.5
  162.0 10.8 %psum.146 = f32[32]{0:T(128)S(1)} all-reduce(f32[32]{0:T(128)S(1)} %multiply_reduce_fusion.12), channel_id=1, replica_groups=mesh['parts'=2,'pix'=4,'par'=4] {'pix'}, use_global_device_ids=true, to_apply=%region_13.14 | all-reduce | flops 32 | bytes 256 | tf_op jit(solution)/shard_map/psum | solution.py:45
  173.9 6.4 %psum.147 = f32[32]{0:T(128)S(1)} all-reduce(f32[32]{0:T(128)S(1)} %get-tuple-element.18), channel_id=1, replica_groups=mesh['parts'=2,'pix'=4,'par'=4] {'par'}, use_global_device_ids=true, to_apply=%region_15.16 | all-reduce | flops 32 | bytes 256 | tf_op jit(solution)/shard_map/psum | solution.py:46
  180.4 6.2 %fusion.34 = f32[32,4096]{1,0:T(8,128)} fusion(bf16[1152,4096]{1,0:T(8,128)(2,1)} %param.2, f32[32,1152]{1,0:T(8,128)S(1)} %multiply_subtract_fusion.7), kind=kOutput, calls=%fused_computation.126 | convolution fusion | flops 302026752 | bytes 10108928 | tf_op jit(solution)/shard_map/dot_general | solution.py:51
  186.9 2.2 collective-permute-start.7
  190.4 3.3 collective-permute-done.6
  194.6 29.7 %all-reduce.20.cloned.1.call-done = f32[32,4096]{1,0:T(8,128)} async-done(((f32[32,4096]{1,0:T(8,128)}), f32[32,4096]{1,0:T(8,128)}) %all-reduce.20.cloned.1.call-update) | async-done | bytes 524304 | tf_op jit(solution)/shard_map/psum | solution.py:51
  225.9 5.7 %psum.149 = f32[32]{0:T(128)S(1)} all-reduce(f32[32]{0:T(128)S(1)} %multiply_reduce_fusion.4), channel_id=1, replica_groups=mesh['parts'=2,'pix'=4,'par'=4] {'par'}, use_global_device_ids=true, to_apply=%region_18.19 | all-reduce | flops 32 | bytes 256 | tf_op jit(solution)/shard_map/psum | solution.py:55
  232.4 6.6 %fusion.56 = f32[32,1152]{1,0:T(8,128)S(1)} fusion(bf16[32,4096]{1,0:T(8,128)(2,1)S(1)} %get-tuple-element.14, bf16[1152,4096]{1,0:T(8,128)(2,1)} %param.2), kind=kOutput, calls=%fused_computation.153 | convolution fusion | flops 301989888 | bytes 9846784 | tf_op jit(solution)/shard_map/dot_general | solution.py:36
  239.0 8.2 %all-gather.2 = f32[128,1152]{1,0:T(8,128)} all-gather(f32[32,1152]{1,0:T(8,128)S(1)} %fusion.56), channel_id=4, replica_groups=mesh['parts'=2,'pix'=4,'par'=4] {'par'}, dimensions={0}, use_global_device_ids=true | all-gather | bytes 737280 | tf_op jit(solution)/shard_map/all_gather | solution.py:39
  248.5 2.3 collective-permute-start.9
  252.2 10.6 %psum.150 = f32[32]{0:T(128)S(1)} all-reduce(f32[32]{0:T(128)S(1)} %multiply_reduce_fusion.11), channel_id=1, replica_groups=mesh['parts'=2,'pix'=4,'par'=4] {'pix'}, use_global_device_ids=true, to_apply=%region_21.22 | all-reduce | flops 32 | bytes 256 | tf_op jit(solution)/shard_map/psum | solution.py:45
  263.9 6.4 %psum.151 = f32[32]{0:T(128)S(1)} all-reduce(f32[32]{0:T(128)S(1)} %get-tuple-element.12), channel_id=1, replica_groups=mesh['parts'=2,'pix'=4,'par'=4] {'par'}, use_global_device_ids=true, to_apply=%region_23.24 | all-reduce | flops 32 | bytes 256 | tf_op jit(solution)/shard_map/psum | solution.py:46
  270.3 6.3 %fusion.32 = f32[32,4096]{1,0:T(8,128)} fusion(bf16[1152,4096]{1,0:T(8,128)(2,1)} %param.2, f32[32,1152]{1,0:T(8,128)S(1)} %multiply_subtract_fusion.7, f32[32,1152]{1,0:T(8,128)S(1)} %reduce_sum.189, f32[32]{0:T(128)S(1)} %get-tuple-element.11), kind=kOutput, calls=%fused_computation.124 | convolution fusion | flops 302100480 | bytes 10256512 | tf_op jit(solution)/shard_map/dot_general | solution.py:51
  276.8 2.2 collective-permute-start.11
  280.4 3.3 collective-permute-done.10
  284.6 29.7 %all-reduce.22.cloned.1.call-done = f32[32,4096]{1,0:T(8,128)} async-done(((f32[32,4096]{1,0:T(8,128)}), f32[32,4096]{1,0:T(8,128)}) %all-reduce.22.cloned.1.call-update) | async-done | bytes 524304 | tf_op jit(solution)/shard_map/psum | solution.py:51
  315.8 5.9 %psum.153 = f32[32]{0:T(128)S(1)} all-reduce(f32[32]{0:T(128)S(1)} %multiply_reduce_fusion.2), channel_id=1, replica_groups=mesh['parts'=2,'pix'=4,'par'=4] {'par'}, use_global_device_ids=true, to_apply=%region_26.27 | all-reduce | flops 32 | bytes 256 | tf_op jit(solution)/shard_map/psum | solution.py:55
  323.1 6.6 %fusion.57 = f32[32,1152]{1,0:T(8,128)S(1)} fusion(bf16[32,4096]{1,0:T(8,128)(2,1)S(1)} %get-tuple-element.8, bf16[1152,4096]{1,0:T(8,128)(2,1)} %param.2), kind=kOutput, calls=%fused_computation.154 | convolution fusion | flops 301989888 | bytes 9846784 | tf_op jit(solution)/shard_map/dot_general | solution.py:36
  329.8 7.8 %all-gather.3 = f32[128,1152]{1,0:T(8,128)S(1)} all-gather(f32[32,1152]{1,0:T(8,128)S(1)} %fusion.57), channel_id=5, replica_groups=mesh['parts'=2,'pix'=4,'par'=4] {'par'}, dimensions={0}, use_global_device_ids=true | all-gather | bytes 737280 | tf_op jit(solution)/shard_map/all_gather | solution.py:39
  339.4 2.3 collective-permute-start.13
  343.1 10.6 %psum.154 = f32[32]{0:T(128)S(1)} all-reduce(f32[32]{0:T(128)S(1)} %multiply_reduce_fusion.10), channel_id=1, replica_groups=mesh['parts'=2,'pix'=4,'par'=4] {'pix'}, use_global_device_ids=true, to_apply=%region_29.30 | all-reduce | flops 32 | bytes 256 | tf_op jit(solution)/shard_map/psum | solution.py:45
  355.5 6.4 %psum.155 = f32[32]{0:T(128)S(1)} all-reduce(f32[32]{0:T(128)S(1)} %get-tuple-element.6), channel_id=1, replica_groups=mesh['parts'=2,'pix'=4,'par'=4] {'par'}, use_global_device_ids=true, to_apply=%region_31.32 | all-reduce | flops 32 | bytes 256 | tf_op jit(solution)/shard_map/psum | solution.py:46
  364.1 6.3 %fusion.30 = f32[32,4096]{1,0:T(8,128)} fusion(bf16[1152,4096]{1,0:T(8,128)(2,1)} %param.2, f32[32,1152]{1,0:T(8,128)S(1)} %multiply_subtract_fusion.5), kind=kOutput, calls=%fused_computation.122 | convolution fusion | flops 302026752 | bytes 10108928 | tf_op jit(solution)/shard_map/dot_general | solution.py:51
  370.6 2.2 collective-permute-start.15
  374.1 3.3 collective-permute-done.14
  378.3 29.8 %all-reduce.24.cloned.1.call-done = f32[32,4096]{1,0:T(8,128)} async-done(((f32[32,4096]{1,0:T(8,128)}), f32[32,4096]{1,0:T(8,128)}) %all-reduce.24.cloned.1.call-update) | async-done | bytes 524304 | tf_op jit(solution)/shard_map/psum | solution.py:51
  409.6 5.7 %psum.157 = f32[32]{0:T(128)S(1)} all-reduce(f32[32]{0:T(128)S(1)} %multiply_reduce_fusion), channel_id=1, replica_groups=mesh['parts'=2,'pix'=4,'par'=4] {'par'}, use_global_device_ids=true, to_apply=%region_34.35 | all-reduce | flops 32 | bytes 256 | tf_op jit(solution)/shard_map/psum | solution.py:55
  416.3 6.6 %fusion.58 = f32[32,1152]{1,0:T(8,128)S(1)} fusion(bf16[32,4096]{1,0:T(8,128)(2,1)S(1)} %fusion.26, bf16[1152,4096]{1,0:T(8,128)(2,1)} %param.2), kind=kOutput, calls=%fused_computation.155 | convolution fusion | flops 301989888 | bytes 9846784 | tf_op jit(solution)/shard_map/dot_general | solution.py:36
  422.8 8.2 %all-gather.4 = f32[128,1152]{1,0:T(8,128)} all-gather(f32[32,1152]{1,0:T(8,128)S(1)} %fusion.58), channel_id=6, replica_groups=mesh['parts'=2,'pix'=4,'par'=4] {'par'}, dimensions={0}, use_global_device_ids=true | all-gather | bytes 737280 | tf_op jit(solution)/shard_map/all_gather | solution.py:39
  432.3 2.3 collective-permute-start.17
  436.0 10.6 %psum.158 = f32[32]{0:T(128)S(1)} all-reduce(f32[32]{0:T(128)S(1)} %multiply_reduce_fusion.9), channel_id=1, replica_groups=mesh['parts'=2,'pix'=4,'par'=4] {'pix'}, use_global_device_ids=true, to_apply=%region_37.38 | all-reduce | flops 32 | bytes 256 | tf_op jit(solution)/shard_map/psum | solution.py:45
  447.8 6.4 %psum.159 = f32[32]{0:T(128)S(1)} all-reduce(f32[32]{0:T(128)S(1)} %fusion.4), channel_id=1, replica_groups=mesh['parts'=2,'pix'=4,'par'=4] {'par'}, use_global_device_ids=true, to_apply=%region_39.40 | all-reduce | flops 32 | bytes 256 | tf_op jit(solution)/shard_map/psum | solution.py:46
  455.0 2.3 multiply_add_fusion
  (161 shorter events, 42.0 us)
Async XLA Ops:
  7.2 47.7 %all-reduce.16.cloned.1.call-start = ((), (), s32[]{:S(2)}) async-start(), calls=%async_computation | async-start | bytes 1048576 | tf_op jit(solution)/shard_map/psum | solution.py:51
  13.5 122.7 %all-reduce.18.cloned.1.call-start = ((), (), s32[]{:S(2)}) async-start(), calls=%async_computation.1 | async-start | bytes 1048576 | tf_op jit(solution)/shard_map/psum | solution.py:51
  70.5 14.3 %collective-permute-start.1 = (f32[32,1,128]{2,1,0:T(1,128)S(1)}, f32[32,1,128]{2,1,0:T(1,128)S(1)}, u32[]{:S(2)}, u32[]{:S(2)}) collective-permute-start(f32[32,1,128]{2,1,0:T(1,128)S(1)} %get-tuple-element.42), channel_id=1, source_target_pairs={{0,1},{1,2},{2,3},{4,5},{5,6},{6,7},{8,9},{9,10},{10,11},{12,13},{... | collective-permute-start | bytes 49160 | tf_op jit(solution)/shard_map/ppermute | solution.py:15
  72.7 12.1 %collective-permute-start = (f32[32,1,128]{2,1,0:T(1,128)S(1)}, f32[32,1,128]{2,1,0:T(1,128)S(1)}, u32[]{:S(2)}, u32[]{:S(2)}) collective-permute-start(f32[32,1,128]{2,1,0:T(1,128)S(1)} %get-tuple-element.43), channel_id=1, source_target_pairs={{1,0},{2,1},{3,2},{5,4},{6,5},{7,6},{9,8},{10,9},{11,10},{13,12},{... | collective-permute-start | bytes 49160 | tf_op jit(solution)/shard_map/ppermute | solution.py:18
  85.3 6.8 %copy-start.11 = (bf16[32,1152]{1,0:T(8,128)(2,1)S(1)}, bf16[32,1152]{1,0:T(8,128)(2,1)}, u32[]{:S(2)}) copy-start(bf16[32,1152]{1,0:T(8,128)(2,1)} %param.3) | copy-start | bytes 221188
  92.1 88.2 %copy-start.14 = (f32[32]{0:T(128)}, f32[32]{0:T(128)S(1)}, u32[]{:S(2)}) copy-start(f32[32]{0:T(128)S(1)} %get-tuple-element.23) | copy-start | bytes 388
  98.4 125.9 %all-reduce.20.cloned.1.call-start = ((), (), s32[]{:S(2)}) async-start(), calls=%async_computation.2 | async-start | bytes 1048576 | tf_op jit(solution)/shard_map/psum | solution.py:51
  98.6 3.6 collective-permute-start.3
  100.9 4.6 collective-permute-start.2
  106.0 37.3 %copy-start = (f32[32,4096]{1,0:T(8,128)S(1)}, f32[32,4096]{1,0:T(8,128)}, u32[]{:S(2)}) copy-start(f32[32,4096]{1,0:T(8,128)} %all-reduce.16.cloned.1.call-done) | copy-start | bytes 1572868
  136.1 7.2 %copy-start.5 = (f32[32,4096]{1,0:T(8,128)S(1)}, f32[32,4096]{1,0:T(8,128)}, u32[]{:S(2)}) copy-start(f32[32,4096]{1,0:T(8,128)} %all-reduce.18.cloned.1.call-done) | copy-start | bytes 1572868
  143.3 36.9 %copy-start.22 = (f32[32]{0:T(128)}, f32[32]{0:T(128)S(1)}, u32[]{:S(2)}) copy-start(f32[32]{0:T(128)S(1)} %psum.145) | copy-start | bytes 388
  158.3 14.5 %collective-permute-start.5 = (f32[32,1,128]{2,1,0:T(1,128)S(1)}, f32[32,1,128]{2,1,0:T(1,128)S(1)}, u32[]{:S(2)}, u32[]{:S(2)}) collective-permute-start(f32[32,1,128]{2,1,0:T(1,128)S(1)} %get-tuple-element.38), channel_id=1, source_target_pairs={{0,1},{1,2},{2,3},{4,5},{5,6},{6,7},{8,9},{9,10},{10,11},{12,13},{... | collective-permute-start | bytes 49160 | tf_op jit(solution)/shard_map/ppermute | solution.py:15
  160.5 12.2 %collective-permute-start.4 = (f32[32,1,128]{2,1,0:T(1,128)S(1)}, f32[32,1,128]{2,1,0:T(1,128)S(1)}, u32[]{:S(2)}, u32[]{:S(2)}) collective-permute-start(f32[32,1,128]{2,1,0:T(1,128)S(1)} %get-tuple-element.39), channel_id=1, source_target_pairs={{1,0},{2,1},{3,2},{5,4},{6,5},{7,6},{9,8},{10,9},{11,10},{13,12},{... | collective-permute-start | bytes 49160 | tf_op jit(solution)/shard_map/ppermute | solution.py:18
  180.3 6.3 %copy-start.18 = (f32[32]{0:T(128)}, f32[32]{0:T(128)S(1)}, u32[]{:S(2)}) copy-start(f32[32]{0:T(128)S(1)} %get-tuple-element.17) | copy-start | bytes 388
  186.6 127.7 %all-reduce.22.cloned.1.call-start = ((), (), s32[]{:S(2)}) async-start(), calls=%async_computation.3 | async-start | bytes 1048576 | tf_op jit(solution)/shard_map/psum | solution.py:51
  186.9 3.6 collective-permute-start.7
  189.1 4.6 collective-permute-start.6
  194.3 37.3 %copy-start.23 = (f32[32]{0:T(128)S(1)}, f32[32]{0:T(128)}, u32[]{:S(2)}) copy-start(f32[32]{0:T(128)} %copy-done.22) | copy-start | bytes 388
  224.3 7.7 %copy-start.4 = (f32[32,4096]{1,0:T(8,128)S(1)}, f32[32,4096]{1,0:T(8,128)}, u32[]{:S(2)}) copy-start(f32[32,4096]{1,0:T(8,128)} %all-reduce.20.cloned.1.call-done) | copy-start | bytes 1572868
  248.5 14.3 %collective-permute-start.9 = (f32[32,1,128]{2,1,0:T(1,128)S(1)}, f32[32,1,128]{2,1,0:T(1,128)S(1)}, u32[]{:S(2)}, u32[]{:S(2)}) collective-permute-start(f32[32,1,128]{2,1,0:T(1,128)S(1)} %get-tuple-element.34), channel_id=1, source_target_pairs={{0,1},{1,2},{2,3},{4,5},{5,6},{6,7},{8,9},{9,10},{10,11},{12,13},{... | collective-permute-start | bytes 49160 | tf_op jit(solution)/shard_map/ppermute | solution.py:15
  250.8 12.0 %collective-permute-start.8 = (f32[32,1,128]{2,1,0:T(1,128)S(1)}, f32[32,1,128]{2,1,0:T(1,128)S(1)}, u32[]{:S(2)}, u32[]{:S(2)}) collective-permute-start(f32[32,1,128]{2,1,0:T(1,128)S(1)} %get-tuple-element.35), channel_id=1, source_target_pairs={{1,0},{2,1},{3,2},{5,4},{6,5},{7,6},{9,8},{10,9},{11,10},{13,12},{... | collective-permute-start | bytes 49160 | tf_op jit(solution)/shard_map/ppermute | solution.py:18
  263.3 7.0 %copy-start.25 = (f32[32]{0:T(128)S(1)}, f32[32]{0:T(128)}, u32[]{:S(2)}) copy-start(f32[32]{0:T(128)} %copy-done.24) | copy-start | bytes 388
  270.3 91.6 %copy-start.12 = (f32[32]{0:T(128)}, f32[32]{0:T(128)S(1)}, u32[]{:S(2)}) copy-start(f32[32]{0:T(128)S(1)} %get-tuple-element.11) | copy-start | bytes 388
  276.6 131.5 %all-reduce.24.cloned.1.call-start = ((), (), s32[]{:S(2)}) async-start(), calls=%async_computation.4 | async-start | bytes 1048576 | tf_op jit(solution)/shard_map/psum | solution.py:51
  276.8 3.6 collective-permute-start.11
  279.1 4.6 collective-permute-start.10
  323.1 6.7 %copy-start.2 = (bf16[32,4096]{1,0:T(8,128)(2,1)}, bf16[32,4096]{1,0:T(8,128)(2,1)S(1)}, u32[]{:S(2)}) copy-start(bf16[32,4096]{1,0:T(8,128)(2,1)S(1)} %get-tuple-element.8) | copy-start | bytes 786436
  338.2 4.7 %copy-start.8 = (f32[32,1152]{1,0:T(8,128)S(1)}, f32[32,1152]{1,0:T(8,128)}, u32[]{:S(2)}) copy-start(f32[32,1152]{1,0:T(8,128)} %reduce_sum.193) | copy-start | bytes 442372
  339.4 14.3 %collective-permute-start.13 = (f32[32,1,128]{2,1,0:T(1,128)S(1)}, f32[32,1,128]{2,1,0:T(1,128)S(1)}, u32[]{:S(2)}, u32[]{:S(2)}) collective-permute-start(f32[32,1,128]{2,1,0:T(1,128)S(1)} %get-tuple-element.30), channel_id=1, source_target_pairs={{0,1},{1,2},{2,3},{4,5},{5,6},{6,7},{8,9},{9,10},{10,11},{12,13},{... | collective-permute-start | bytes 49160 | tf_op jit(solution)/shard_map/ppermute | solution.py:15
  341.7 12.0 %collective-permute-start.12 = (f32[32,1,128]{2,1,0:T(1,128)S(1)}, f32[32,1,128]{2,1,0:T(1,128)S(1)}, u32[]{:S(2)}, u32[]{:S(2)}) collective-permute-start(f32[32,1,128]{2,1,0:T(1,128)S(1)} %get-tuple-element.31), channel_id=1, source_target_pairs={{1,0},{2,1},{3,2},{5,4},{6,5},{7,6},{9,8},{10,9},{11,10},{13,12},{... | collective-permute-start | bytes 49160 | tf_op jit(solution)/shard_map/ppermute | solution.py:18
  363.5 0.7 copy-start.6
  364.1 6.3 %copy-start.3 = (f32[32,32,128]{2,1,0:T(8,128)S(1)}, f32[32,32,128]{2,1,0:T(8,128)}, u32[]{:S(2)}) copy-start(f32[32,32,128]{2,1,0:T(8,128)} %get-tuple-element.7) | copy-start | bytes 1572868
  370.6 3.6 collective-permute-start.15
  372.8 4.6 collective-permute-start.14
  408.1 7.8 %copy-start.1 = (f32[32,4096]{1,0:T(8,128)S(1)}, f32[32,4096]{1,0:T(8,128)}, u32[]{:S(2)}) copy-start(f32[32,4096]{1,0:T(8,128)} %all-reduce.24.cloned.1.call-done) | copy-start | bytes 1572868
  415.3 7.5 %copy-start.26 = (f32[32]{0:T(128)}, f32[32]{0:T(128)S(1)}, u32[]{:S(2)}) copy-start(f32[32]{0:T(128)S(1)} %psum.157) | copy-start | bytes 388
  432.2 3.9 copy-start.9
  432.3 14.3 %collective-permute-start.17 = (f32[32,1,128]{2,1,0:T(1,128)S(1)}, f32[32,1,128]{2,1,0:T(1,128)S(1)}, u32[]{:S(2)}, u32[]{:S(2)}) collective-permute-start(f32[32,1,128]{2,1,0:T(1,128)S(1)} %get-tuple-element.26), channel_id=1, source_target_pairs={{0,1},{1,2},{2,3},{4,5},{5,6},{6,7},{8,9},{9,10},{10,11},{12,13},{... | collective-permute-start | bytes 49160 | tf_op jit(solution)/shard_map/ppermute | solution.py:15
  434.6 12.1 %collective-permute-start.16 = (f32[32,1,128]{2,1,0:T(1,128)S(1)}, f32[32,1,128]{2,1,0:T(1,128)S(1)}, u32[]{:S(2)}, u32[]{:S(2)}) collective-permute-start(f32[32,1,128]{2,1,0:T(1,128)S(1)} %get-tuple-element.27), channel_id=1, source_target_pairs={{1,0},{2,1},{3,2},{5,4},{6,5},{7,6},{9,8},{10,9},{11,10},{13,12},{... | collective-permute-start | bytes 49160 | tf_op jit(solution)/shard_map/ppermute | solution.py:18
  446.6 7.6 %copy-start.27 = (f32[32]{0:T(128)S(1)}, f32[32]{0:T(128)}, u32[]{:S(2)}) copy-start(f32[32]{0:T(128)} %copy-done.26) | copy-start | bytes 388
  446.6 7.6 %copy-start.7 = (f32[32,1152]{1,0:T(8,128)S(1)}, f32[32,1152]{1,0:T(8,128)}, u32[]{:S(2)}) copy-start(f32[32,1152]{1,0:T(8,128)} %copy-done.6) | copy-start | bytes 442372
  446.6 7.6 %copy-start.10 = (f32[32,1152]{1,0:T(8,128)S(1)}, f32[32,1152]{1,0:T(8,128)}, u32[]{:S(2)}) copy-start(f32[32,1152]{1,0:T(8,128)} %copy-done.9) | copy-start | bytes 442372
  447.2 7.8 %copy-start.13 = (f32[32]{0:T(128)S(1)}, f32[32]{0:T(128)}, u32[]{:S(2)}) copy-start(f32[32]{0:T(128)} %copy-done.12) | copy-start | bytes 388
  447.2 7.8 %copy-start.15 = (f32[32]{0:T(128)S(1)}, f32[32]{0:T(128)}, u32[]{:S(2)}) copy-start(f32[32]{0:T(128)} %copy-done.14) | copy-start | bytes 388
  447.2 7.8 %copy-start.17 = (f32[32]{0:T(128)S(1)}, f32[32]{0:T(128)}, u32[]{:S(2)}) copy-start(f32[32]{0:T(128)} %copy-done.16) | copy-start | bytes 388
  447.2 7.8 %copy-start.19 = (f32[32]{0:T(128)S(1)}, f32[32]{0:T(128)}, u32[]{:S(2)}) copy-start(f32[32]{0:T(128)} %copy-done.18) | copy-start | bytes 388
  447.3 7.8 %copy-start.21 = (f32[32]{0:T(128)S(1)}, f32[32]{0:T(128)}, u32[]{:S(2)}) copy-start(f32[32]{0:T(128)} %copy-done.20) | copy-start | bytes 388
  (3 other events, 1.6 us)
Sparse Core Ops, SparseCore 0:
  13.6 41.2 all-reduce.15
  98.6 37.5 all-reduce.17
  186.8 37.5 all-reduce.19
  276.8 37.5 all-reduce.21
  370.5 37.5 all-reduce.23
